TPU v7x, 32 devices: a whole 2x2x4 slice. The times are simulated.
32 devices in a mesh: ctx: 16 (over z, x, core), head: 2 (over y).
Axes of the slice: x: 2, y: 2, z: 4, core: 2. Of those that a mesh axis runs over, the one named last changes fastest.
Arguments:
- queries: bfloat16 [256, 4096], P('ctx', 'head'), may hold values from -1500 to 1500
- cache_keys: bfloat16 [65536, 2048], P('ctx', 'head'), may hold values from -15 to 15
- prefix_cache_values: bfloat16 [65536, 2048], P('ctx', 'head'), may hold values from -6 to 6
- incoming_keys: bfloat16 [256, 2048], P('ctx', 'head'), may hold values from -15 to 15
- incoming_values: bfloat16 [256, 2048], P('ctx', 'head'), may hold values from -6 to 6
Outputs:
- attended: bfloat16 [256, 4096], P('ctx', 'head')
All inputs are finite; a program needn't handle non-finite values.
Results may differ from a plain program's by a relative error of at most 0.005.
Values may be sent and summed in bfloat16 or wider, within the bound.
A program may use at most 64 MiB of HBM per device.

v0:
```python
import functools
import math

import jax
import jax.numpy as jnp
from jax import lax
from jax.experimental import pallas as pl
from jax.experimental.pallas import tpu as pltpu
from jax.sharding import PartitionSpec as P

HEAD_SIZE = 128
LANES = 128
SUBLANES = 8
SUM_ROW = 4
TILE_ROWS = 256
BLOCK_KEYS = 1024
PIECE_KEYS = 256
EXP2_SCALE = 168.0 ** (-0.5) * math.log2(math.e)
MASKED = -1e30
BF16, F32 = jnp.bfloat16, jnp.float32


def nt_dot(a, b):
    return lax.dot_general(a, b, (((1,), (1,)), ((), ())), preferred_element_type=F32)


def tn_dot(a, b):
    return lax.dot_general(a, b, (((0,), (0,)), ((), ())), preferred_element_type=F32)


def fold(x, op):
    parts = [x[i] for i in range(x.shape[0])]
    while len(parts) > 1:
        parts = [op(*parts[i:i + 2]) if i + 1 < len(parts) else parts[i] for i in range(0, len(parts), 2)]
    return parts[0]


def kernel(
    devices, heads, group, own, block,
    q_hbm, k_hbm, v_hbm, fk_hbm, fv_hbm, out_ref,
    qown, qbuf, kbuf, vbuf, fkbuf, fvbuf, scores_even, scores_odd, fresh_scores, relative,
    block_max, row_max, row_sum, acc, obuf, xbuf, sbuf, mbuf, rbuf, rmbuf,
    q_sem, k_sem, v_sem, f_sem, gather_send, gather_recv, relay_send, relay_recv,
    x_send, x_recv, o_send, o_recv, m_send, m_recv,
):
    pairs = devices // 2
    each = group * own
    tile_pairs = qbuf.shape[3]
    tiles = qbuf.shape[1]
    rows = 2 * tile_pairs * each
    blocks = kbuf.shape[1] // block
    units = heads * tiles
    early = heads // 2 if tiles > 1 else heads
    me = lax.axis_index("ctx")
    core, pair = lax.rem(me, 2), lax.div(me, 2)
    my_tile, my_place = lax.div(pair, tile_pairs), lax.rem(pair, tile_pairs)

    def unit(u):
        far = u - early
        late = u - heads * (tiles - 1)
        is_early, is_late = u < early, u >= early + heads * (tiles - 1)
        far_step, far_head = 1 + lax.div(jnp.maximum(far, 0), heads), lax.rem(jnp.maximum(far, 0), heads)
        step = jnp.where(is_early | is_late, 0, far_step)
        h = jnp.where(is_early, u, jnp.where(is_late, late, far_head))
        return h, step, lax.rem(my_tile + step, tiles)

    def head_columns(h):
        return pl.ds(pl.multiple_of(h * HEAD_SIZE, HEAD_SIZE), HEAD_SIZE)

    def q_copy(h, g):
        columns = pl.ds((h * group + g) * HEAD_SIZE, HEAD_SIZE)
        return pltpu.make_async_copy(q_hbm.at[:, columns], qown.at[h, pl.ds(g * own, own)], q_sem.at[h, g])

    def q_place(h, g):
        columns = pl.ds((h * group + g) * HEAD_SIZE, HEAD_SIZE)
        return pltpu.make_async_copy(
            q_hbm.at[:, columns], qbuf.at[h, my_tile, core, my_place, pl.ds(g * own, own)],
            gather_recv.at[h, my_tile],
        )

    def k_copy(h):
        return pltpu.make_async_copy(k_hbm.at[:, head_columns(h)], kbuf.at[h], k_sem.at[h])

    def v_copy(h):
        return pltpu.make_async_copy(v_hbm.at[:, head_columns(h)], vbuf.at[h], v_sem.at[h])

    fk_copy = pltpu.make_async_copy(fk_hbm, fkbuf, f_sem.at[0])
    fv_copy = pltpu.make_async_copy(fv_hbm, fvbuf, f_sem.at[1])

    for h in range(heads):
        for g in range(group):
            q_copy(h, g).start()

    barrier = pltpu.get_barrier_semaphore()

    def greet(step, _):
        peer = lax.rem(me + step, devices)
        pl.semaphore_signal(barrier, inc=1, device_id={"ctx": peer}, device_id_type=pl.DeviceIdType.MESH)
        return 0

    lax.fori_loop(1, devices, greet, 0)
    for h in range(heads):
        for g in range(group):
            q_place(h, g).start()
    k_copy(0).start()
    fk_copy.start()
    fv_copy.start()
    v_copy(0).start()
    for h in range(1, heads):
        k_copy(h).start()
        v_copy(h).start()

    row = lax.broadcasted_iota(jnp.int32, (own, rows), 1)
    key = lax.broadcasted_iota(jnp.int32, (own, rows), 0)
    half = tile_pairs * each
    device = lax.div(lax.rem(row, half), each) * 2 + lax.div(row, half)
    relative[...] = device * own + lax.rem(row, own) - key

    for h in range(heads):
        for g in range(group):
            q_copy(h, g).wait()
    pl.semaphore_wait(barrier, devices - 1)

    def gather_copy(h, peer_pair):
        return pltpu.make_async_remote_copy(
            src_ref=qown.at[h], dst_ref=qbuf.at[h, my_tile, core, my_place],
            send_sem=gather_send.at[h], recv_sem=gather_recv.at[h, my_tile],
            device_id={"ctx": peer_pair * 2 + core}, device_id_type=pl.DeviceIdType.MESH,
        )

    def gather(u, _):
        h, step, tile = unit(u)

        def send(j, _):
            gather_copy(h, tile * tile_pairs + lax.rem(my_place + j, tile_pairs)).start()
            return 0

        return lax.fori_loop(jnp.where(step == 0, 1, 0), tile_pairs, send, 0)

    lax.fori_loop(0, units, gather, 0)

    def relay_copy(h, tile):
        mine = qbuf.at[h, tile, core]
        return pltpu.make_async_remote_copy(
            src_ref=mine, dst_ref=mine, send_sem=relay_send.at[h, tile], recv_sem=relay_recv.at[h, tile],
            device_id={"ctx": pair * 2 + 1 - core}, device_id_type=pl.DeviceIdType.MESH,
        )

    def relay(u):
        h, _, tile = unit(u)
        mine = qbuf.at[h, tile, core]
        pltpu.make_async_copy(mine, mine, gather_recv.at[h, tile]).wait()
        relay_copy(h, tile).start()

    def await_queries(u):
        h, step, tile = unit(u)
        relay_copy(h, tile).wait_recv()

        @pl.when((u < early) | ((step == 1) & (h >= early)))
        def _():
            k_copy(h).wait()
            v_copy(h).wait()

    score_slots = (scores_even, scores_odd)

    def score_piece(h, queries, b, j):
        keys = kbuf[h, pl.ds(b * block + j * PIECE_KEYS, PIECE_KEYS), :]
        s = nt_dot(keys, queries)
        score_slots[b % 2][pl.ds(j * PIECE_KEYS, PIECE_KEYS), :] = s
        return fold(s.reshape(PIECE_KEYS // SUBLANES, SUBLANES, rows), jnp.maximum)

    def score_fresh(h, tile, queries):
        s = nt_dot(fkbuf[:, head_columns(h)], queries)
        seen = relative[...] >= (me - tile * 2 * tile_pairs) * own
        s = jnp.where(seen, s, MASKED)
        fresh_scores[...] = s
        return fold(s.reshape(own // SUBLANES, SUBLANES, rows), jnp.maximum)

    def segment(values, scores):
        if values is not None:
            vh, vb = values
            top = jnp.max(block_max[vb % 2], axis=0, keepdims=True)
            if vb > 0:
                before = row_max[0:1]
                top = jnp.maximum(before, top)
                decay = jnp.exp2((before - top) * EXP2_SCALE)
            row_max[0:1] = top
            top8 = jnp.broadcast_to(top, (SUBLANES, rows))
            weights, sums = [], []
        if scores is not None:
            sh, tile, sb = scores
            queries = qbuf[sh, tile].reshape(rows, HEAD_SIZE)
            tops = []
        for j in range(block // PIECE_KEYS):
            if values is not None:
                s = score_slots[vb % 2][pl.ds(j * PIECE_KEYS, PIECE_KEYS), :]
                s = s.reshape(PIECE_KEYS // SUBLANES, SUBLANES, rows)
                p = jnp.exp2((s - top8[None]) * EXP2_SCALE)
                sums.append(fold(p, jnp.add))
                weights.append(p.reshape(PIECE_KEYS, rows).astype(BF16))
            if scores is not None:
                tops.append(score_piece(sh, queries, sb, j))
        if scores is not None:
            if sb == 0:
                tops.append(score_fresh(sh, tile, queries))
            block_max[sb % 2] = functools.reduce(jnp.maximum, tops)
        if values is not None:
            out = tn_dot(vbuf[vh, pl.ds(vb * block, block), :], jnp.concatenate(weights, axis=0))
            if vb == 0:
                s = fresh_scores[...].reshape(own // SUBLANES, SUBLANES, rows)
                p = jnp.exp2((s - top8[None]) * EXP2_SCALE)
                sums.append(fold(p, jnp.add))
                out = out + tn_dot(fvbuf[:, head_columns(vh)], p.reshape(own, rows).astype(BF16))
            total = functools.reduce(jnp.add, sums)
            if vb == 0:
                row_sum[...] = total
                acc[...] = out
            else:
                row_sum[...] = row_sum[...] * decay + total
                acc[...] = acc[...] * decay + out

    def close(u):
        total = jnp.sum(row_sum[...], axis=0, keepdims=True)
        upper = lax.broadcasted_iota(jnp.int32, (SUBLANES, half), 0) < SUM_ROW
        for c in range(2):
            span = slice(c * half, (c + 1) * half)
            obuf[u, c, :HEAD_SIZE] = acc[:, span]
            obuf[u, c, HEAD_SIZE:] = jnp.where(upper, row_max[0:1, span], total[:, span])

    def exchange_copy(u):
        return pltpu.make_async_remote_copy(
            src_ref=obuf.at[u, 1 - core], dst_ref=xbuf.at[u], send_sem=x_send.at[u], recv_sem=x_recv.at[u],
            device_id={"ctx": pair * 2 + 1 - core}, device_id_type=pl.DeviceIdType.MESH,
        )

    def merge(u):
        own_part, other_part = obuf[u, core, HEAD_SIZE:], xbuf[u, HEAD_SIZE:]
        top_a, top_b = own_part[:1], other_part[:1]
        sum_a, sum_b = own_part[SUM_ROW:SUM_ROW + 1], other_part[SUM_ROW:SUM_ROW + 1]
        top = jnp.maximum(top_a, top_b)
        scale_a = jnp.exp2((top_a - top) * EXP2_SCALE)
        scale_b = jnp.exp2((top_b - top) * EXP2_SCALE)
        total = sum_a * scale_a + sum_b * scale_b
        out = obuf[u, core, :HEAD_SIZE] * (scale_a / total) + xbuf[u, :HEAD_SIZE] * (scale_b / total)
        sbuf[u] = out.T.astype(BF16).reshape(tile_pairs, each, HEAD_SIZE)
        mbuf[u, 0:1] = top
        mbuf[u, 1:2] = total

    def out_copy(u, h, tile, place):
        return pltpu.make_async_remote_copy(
            src_ref=sbuf.at[u, place], dst_ref=rbuf.at[h, pair], send_sem=o_send.at[h], recv_sem=o_recv.at[h],
            device_id={"ctx": (tile * tile_pairs + place) * 2 + core}, device_id_type=pl.DeviceIdType.MESH,
        )

    def sums_copy(u, h, tile, place):
        return pltpu.make_async_remote_copy(
            src_ref=mbuf.at[u], dst_ref=rmbuf.at[h, pair], send_sem=m_send.at[h], recv_sem=m_recv.at[h],
            device_id={"ctx": (tile * tile_pairs + place) * 2 + core}, device_id_type=pl.DeviceIdType.MESH,
        )

    def send_out(u):
        h, step, tile = unit(u)

        def send(j, _):
            place = lax.rem(my_place + j, tile_pairs)
            sums_copy(u, h, tile, place).start()
            out_copy(u, h, tile, place).start()
            return 0

        lax.fori_loop(jnp.where(step == 0, 1, 0), tile_pairs, send, 0)

        @pl.when(step == 0)
        def _():
            rbuf[h, pair] = sbuf[u, my_place]
            rmbuf[h, pair] = mbuf[u]

    def incoming(ref, h, sem):
        part = ref.at[h, pl.ds(0, pairs - 1)]
        return pltpu.make_async_copy(part, part, sem.at[h])

    def combine(h):
        incoming(rmbuf, h, m_recv).wait()
        incoming(rbuf, h, o_recv).wait()
        tops, sums = rmbuf[h, :, 0, :], rmbuf[h, :, 1, :]
        weights = jnp.exp2((tops - jnp.max(tops, axis=0, keepdims=True)) * EXP2_SCALE) * sums
        weights = weights / jnp.sum(weights, axis=0, keepdims=True)
        mine = jnp.zeros((pairs, each), F32)
        for place in range(tile_pairs):
            mine = jnp.where(my_place == place, weights[:, place * each:(place + 1) * each], mine)
        diagonal = lax.broadcasted_iota(jnp.int32, (each, each), 0) == lax.broadcasted_iota(
            jnp.int32, (each, each), 1
        )
        result = jnp.zeros((each, HEAD_SIZE), F32)
        for source in range(pairs):
            line = jnp.broadcast_to(mine[source:source + 1, :], (each, each))
            column = jnp.sum(jnp.where(diagonal, line, 0.0), axis=1, keepdims=True)
            result = result + column * rbuf[h, source].astype(F32)
        for g in range(group):
            columns = pl.ds(pl.multiple_of((h * group + g) * HEAD_SIZE, HEAD_SIZE), HEAD_SIZE)
            out_ref[:, columns] = result[g * own:(g + 1) * own].astype(out_ref.dtype)

    def body(u, first=False, second=False):
        h, _, tile = unit(u)
        await_queries(u)
        if not first and not second:
            exchange_copy(u - 2).wait_recv()

        @pl.when(u + 2 < units)
        def _():
            relay(u + 2)

        if first:
            segment(None, (h, tile, 0))
        else:
            segment((unit(u - 1)[0], blocks - 1), (h, tile, 0))
            close(u - 1)
            if not second:
                merge(u - 2)
        for b in range(1, blocks):
            segment((h, b - 1), (h, tile, b))
            if b == 1 and not first:
                exchange_copy(u - 1).start()
                if not second:
                    send_out(u - 2)

    relay(0)
    if units > 1:
        relay(1)
    fk_copy.wait()
    fv_copy.wait()
    body(jnp.int32(0), first=True)
    if units > 1:
        body(jnp.int32(1), second=True)
    lax.fori_loop(2, units, lambda u, _: (body(u), 0)[1], 0)
    last = units - 1
    if units > 1:
        exchange_copy(last - 1).wait_recv()
        merge(last - 1)
    segment((unit(jnp.int32(last))[0], blocks - 1), None)
    close(last)
    exchange_copy(last).start()
    if units > 1:
        send_out(jnp.int32(last - 1))
    lax.fori_loop(0, heads // 2, lambda h, _: (combine(h), 0)[1], 0)
    exchange_copy(last).wait_recv()
    merge(last)
    send_out(jnp.int32(last))
    lax.fori_loop(heads // 2, heads, lambda h, _: (combine(h), 0)[1], 0)

    def drain(h, _):
        incoming(rbuf, h, gather_send).wait()
        incoming(rmbuf, h, m_send).wait()
        incoming(rbuf, h, o_send).wait()
        return 0

    def drain_unit(u, _):
        h, _, tile = unit(u)
        relay_copy(h, tile).wait_send()
        exchange_copy(u).wait_send()
        return 0

    lax.fori_loop(0, heads, drain, 0)
    lax.fori_loop(0, units, drain_unit, 0)


def solution(mesh):
    devices = mesh.shape["ctx"]

    def shards(queries, cache_keys, prefix_values, incoming_keys, incoming_values):
        own = queries.shape[0]
        heads = cache_keys.shape[1] // HEAD_SIZE
        group = queries.shape[1] // cache_keys.shape[1]
        depth = cache_keys.shape[0]
        each = group * own
        pairs = devices // 2
        tile_pairs = min(pairs, TILE_ROWS // (2 * each))
        tiles = pairs // tile_pairs
        rows = 2 * tile_pairs * each
        units = heads * tiles
        block = min(BLOCK_KEYS, depth // 2)
        dma = pltpu.SemaphoreType.DMA
        return pl.pallas_call(
            functools.partial(kernel, devices, heads, group, own, block),
            out_shape=jax.ShapeDtypeStruct(queries.shape, queries.dtype),
            in_specs=[pl.BlockSpec(memory_space=pl.ANY)] * 5,
            out_specs=pl.BlockSpec(memory_space=pltpu.VMEM),
            scratch_shapes=[
                pltpu.VMEM((heads, each, HEAD_SIZE), BF16),
                pltpu.VMEM((heads, tiles, 2, tile_pairs, each, HEAD_SIZE), BF16),
                pltpu.VMEM((heads, depth, HEAD_SIZE), BF16),
                pltpu.VMEM((heads, depth, HEAD_SIZE), BF16),
                pltpu.VMEM((own, heads * HEAD_SIZE), BF16),
                pltpu.VMEM((own, heads * HEAD_SIZE), BF16),
                pltpu.VMEM((block, rows), F32),
                pltpu.VMEM((block, rows), F32),
                pltpu.VMEM((own, rows), F32),
                pltpu.VMEM((own, rows), jnp.int32),
                pltpu.VMEM((2, SUBLANES, rows), F32),
                pltpu.VMEM((SUBLANES, rows), F32),
                pltpu.VMEM((SUBLANES, rows), F32),
                pltpu.VMEM((HEAD_SIZE, rows), F32),
                pltpu.VMEM((units, 2, HEAD_SIZE + SUBLANES, rows // 2), F32),
                pltpu.VMEM((units, HEAD_SIZE + SUBLANES, rows // 2), F32),
                pltpu.VMEM((units, tile_pairs, each, HEAD_SIZE), BF16),
                pltpu.VMEM((units, 2, rows // 2), F32),
                pltpu.VMEM((heads, pairs, each, HEAD_SIZE), BF16),
                pltpu.VMEM((heads, pairs, 2, rows // 2), F32),
                dma((heads, group)), dma((heads,)), dma((heads,)), dma((2,)),
                dma((heads,)), dma((heads, tiles)), dma((heads, tiles)), dma((heads, tiles)),
                dma((units,)), dma((units,)), dma((heads,)), dma((heads,)), dma((heads,)), dma((heads,)),
            ],
            compiler_params=pltpu.CompilerParams(
                collective_id=0, has_side_effects=True, vmem_limit_bytes=60 * 1024 * 1024
            ),
        )(queries, cache_keys, prefix_values, incoming_keys, incoming_values)

    spec = P("ctx", "head")
    return jax.shard_map(
        shards, mesh=mesh, in_specs=(spec,) * 5, out_specs=spec, check_vma=False
    )
```

profile of v0, /device:TPU:0, one launch (start us, length us, event | category | flops | bytes accessed | tf_op | source)
XLA Modules:
  0.0 48.1 jit_solution(12441559095501466425)
XLA Ops:
  0.0 46.6 %shard_map.55 = bf16[16,2048]{1,0:T(8,128)(2,1)} custom-call(bf16[16,2048]{1,0:T(8,128)(2,1)} %q_hbm.1, bf16[4096,1024]{1,0:T(8,128)(2,1)} %k_hbm.1, bf16[4096,1024]{1,0:T(8,128)(2,1)} %v_hbm.1, bf16[16,1024]{1,0:T(8,128)(2,1)} %fk_hbm.1, bf16[16,1024]{1,0:T(8,128)(2,1)} %fv_hbm.1), custom_call_target="tpu_custom_call" | custom-call | tf_op jit(solution)/shard_map/pallas_call | solution.py:382
  46.6 1.5 %copy.7 = bf16[16,2048]{1,0:T(8,128)(2,1)} copy(bf16[16,2048]{1,0:T(8,128)(2,1)} %shard_map.55) | data formatting | bytes 131072
where the time goes:
time: 48.2 us; the launch traced here: 48.1 us
  Pallas kernels  46.6 us (97%)
  local copies, waits for them, and re-layouts  1.47 us (3%)
    pallas_call x1, Pallas kernels, shards(): pl.pallas_call(functools.partial(kernel, devices, heads, group, own, bloc...  46.6 us
    unnamed x1, local copies, waits for them, and re-layouts  1.47 us

commit v1 on v0

v1 whole, which is shorter than its diff:
```python
import functools
import math

import jax
import jax.numpy as jnp
from jax import lax
from jax.experimental import pallas as pl
from jax.experimental.pallas import tpu as pltpu
from jax.sharding import PartitionSpec as P

HEAD_SIZE = 128
LANES = 128
SUBLANES = 8
SUM_ROW = 4
TILE_ROWS = 256
BLOCK_KEYS = 1024
PIECE_KEYS = 256
EXP2_SCALE = 168.0 ** (-0.5) * math.log2(math.e)
MASKED = -1e30
BF16, F32 = jnp.bfloat16, jnp.float32


def nt_dot(a, b):
    return lax.dot_general(a, b, (((1,), (1,)), ((), ())), preferred_element_type=F32)


def tn_dot(a, b):
    return lax.dot_general(a, b, (((0,), (0,)), ((), ())), preferred_element_type=F32)


def fold(x, op):
    parts = [x[i] for i in range(x.shape[0])]
    while len(parts) > 1:
        parts = [op(*parts[i:i + 2]) if i + 1 < len(parts) else parts[i] for i in range(0, len(parts), 2)]
    return parts[0]


def kernel(
    devices, heads, group, own, block,
    q_hbm, k_hbm, v_hbm, fk_hbm, fv_hbm, out_ref,
    qbuf, kbuf, vbuf, fkbuf, fvbuf, scores_even, scores_odd, fresh_scores, relative,
    block_max, row_max, row_sum, acc, obuf, xbuf, sbuf, smbuf, nbuf, nmbuf, hbuf, hmbuf, fbuf, fmbuf,
    k_sem, v_sem, f_sem, ready, block_recv, gather_recv, relay_recv, x_recv, n_recv, nm_recv, far_recv, farm_recv,
    far_query_send, gather_send, relay_send, x_send, n_send, nm_send, far_send, farm_send,
):
    tiles, tile_pairs = qbuf.shape[1], qbuf.shape[3]
    each = group * own
    half = tile_pairs * each
    rows = 2 * half
    tile_devices = 2 * tile_pairs
    blocks = kbuf.shape[1] // block
    units = heads * tiles
    early = heads // 2 if tiles > 1 else heads
    late = early + heads * (tiles - 1)
    me = lax.axis_index("ctx")
    core, pair = lax.rem(me, 2), lax.div(me, 2)
    my_tile, my_place = lax.div(pair, tile_pairs), lax.rem(pair, tile_pairs)

    def is_far(u):
        return (u >= early) & (u < late)

    def unit(u):
        far = jnp.maximum(u - early, 0)
        near = jnp.where(u < early, u, u - heads * (tiles - 1))
        h = jnp.where(is_far(u), lax.rem(far, heads), near)
        step = jnp.where(is_far(u), 1 + lax.div(far, heads), 0)
        return h, step, lax.rem(my_tile + step, tiles)

    def near_unit(h):
        return jnp.where(h < early, h, h + heads * (tiles - 1))

    def neighbour(j):
        return {"ctx": (my_tile * tile_pairs + lax.rem(my_place + j, tile_pairs)) * 2 + core}

    sibling = {"ctx": pair * 2 + 1 - core}

    def partner(tile):
        return {"ctx": (tile * tile_pairs + my_place) * 2 + core}

    def remote(src, dst, send_sem, recv_sem, device):
        return pltpu.make_async_remote_copy(
            src_ref=src, dst_ref=dst, send_sem=send_sem, recv_sem=recv_sem,
            device_id=device, device_id_type=pl.DeviceIdType.MESH,
        )

    def await_bytes(ref, sem):
        pltpu.make_async_copy(ref, ref, sem).wait()

    def head_columns(h):
        return pl.ds(pl.multiple_of(h * HEAD_SIZE, HEAD_SIZE), HEAD_SIZE)

    def k_copy(h):
        return pltpu.make_async_copy(k_hbm.at[:, head_columns(h)], kbuf.at[h], k_sem.at[h])

    def v_copy(h):
        return pltpu.make_async_copy(v_hbm.at[:, head_columns(h)], vbuf.at[h], v_sem.at[h])

    fk_copy = pltpu.make_async_copy(fk_hbm, fkbuf, f_sem.at[0])
    fv_copy = pltpu.make_async_copy(fv_hbm, fvbuf, f_sem.at[1])

    barrier = pltpu.get_barrier_semaphore()

    def signal(sem, device):
        pl.semaphore_signal(sem, inc=1, device_id=device, device_id_type=pl.DeviceIdType.MESH)

    for j in range(1, tile_devices):
        signal(barrier, {"ctx": my_tile * tile_devices + lax.rem(lax.rem(me, tile_devices) + j, tile_devices)})
    lax.fori_loop(my_tile + 1, tiles, lambda t, _: (signal(barrier, partner(t)), 0)[1], 0)

    for h in range(heads):
        for g in range(group):
            columns = pl.ds((h * group + g) * HEAD_SIZE, HEAD_SIZE)
            pltpu.make_async_copy(
                q_hbm.at[:, columns], qbuf.at[h, my_tile, core, my_place, pl.ds(g * own, own)],
                block_recv.at[h, my_tile],
            ).start()
    k_copy(0).start()
    fk_copy.start()
    fv_copy.start()
    v_copy(0).start()

    row = lax.broadcasted_iota(jnp.int32, (own, rows), 1)
    key = lax.broadcasted_iota(jnp.int32, (own, rows), 0)
    device = lax.div(lax.rem(row, half), each) * 2 + lax.div(row, half)
    relative[...] = device * own + lax.rem(row, own) - key

    def await_block(h, tile):
        await_bytes(qbuf.at[h, tile, core, my_place], block_recv.at[h, tile])

    def forward(h, tile):
        mine = qbuf.at[h, tile, core, my_place]
        for j in range(1, tile_pairs):
            remote(mine, mine, gather_send.at[0], gather_recv.at[h, tile], neighbour(j)).start()

    def relay_copy(h, tile):
        mine = qbuf.at[h, tile, core]
        return remote(mine, mine, relay_send.at[0], relay_recv.at[h, tile], sibling)

    def relay(h, tile):
        await_bytes(qbuf.at[h, tile, core, pl.ds(0, tile_pairs - 1)], gather_recv.at[h, tile])
        relay_copy(h, tile).start()

    def await_queries(u):
        h, step, tile = unit(u)
        relay_copy(h, tile).wait_recv()

        @pl.when((u < early) | ((step == 1) & (h >= early)))
        def _():
            k_copy(h).wait()
            v_copy(h).wait()

    score_slots = (scores_even, scores_odd)

    def score_piece(h, queries, b, j):
        keys = kbuf[h, pl.ds(b * block + j * PIECE_KEYS, PIECE_KEYS), :]
        s = nt_dot(keys, queries)
        score_slots[b % 2][pl.ds(j * PIECE_KEYS, PIECE_KEYS), :] = s
        return fold(s.reshape(PIECE_KEYS // SUBLANES, SUBLANES, rows), jnp.maximum)

    def score_fresh(h, tile, queries):
        s = nt_dot(fkbuf[:, head_columns(h)], queries)
        seen = relative[...] >= (me - tile * tile_devices) * own
        s = jnp.where(seen, s, MASKED)
        fresh_scores[...] = s
        return fold(s.reshape(own // SUBLANES, SUBLANES, rows), jnp.maximum)

    def segment(values, scores, finish=None):
        if values is not None:
            vh, vb = values
            top = jnp.max(block_max[vb % 2], axis=0, keepdims=True)
            if vb > 0:
                before = row_max[0:1]
                top = jnp.maximum(before, top)
                decay = jnp.exp2((before - top) * EXP2_SCALE)
            row_max[0:1] = top
            top8 = jnp.broadcast_to(top, (SUBLANES, rows))
            weights, sums = [], []
        if scores is not None:
            sh, tile, sb = scores
            queries = qbuf[sh, tile].reshape(rows, HEAD_SIZE)
            tops = []
        for j in range(block // PIECE_KEYS):
            if values is not None:
                s = score_slots[vb % 2][pl.ds(j * PIECE_KEYS, PIECE_KEYS), :]
                s = s.reshape(PIECE_KEYS // SUBLANES, SUBLANES, rows)
                p = jnp.exp2((s - top8[None]) * EXP2_SCALE)
                sums.append(fold(p, jnp.add))
                weights.append(p.reshape(PIECE_KEYS, rows).astype(BF16))
            if scores is not None:
                tops.append(score_piece(sh, queries, sb, j))
        if scores is not None:
            if sb == 0:
                tops.append(score_fresh(sh, tile, queries))
            block_max[sb % 2] = functools.reduce(jnp.maximum, tops)
        if values is not None:
            out = tn_dot(vbuf[vh, pl.ds(vb * block, block), :], jnp.concatenate(weights, axis=0))
            if vb == 0:
                s = fresh_scores[...].reshape(own // SUBLANES, SUBLANES, rows)
                p = jnp.exp2((s - top8[None]) * EXP2_SCALE)
                sums.append(fold(p, jnp.add))
                out = out + tn_dot(fvbuf[:, head_columns(vh)], p.reshape(own, rows).astype(BF16))
            total = functools.reduce(jnp.add, sums)
            if vb > 0:
                total = row_sum[...] * decay + total
                out = acc[...] * decay + out
            if finish is None:
                row_sum[...] = total
                acc[...] = out
            else:
                total = jnp.sum(total, axis=0, keepdims=True)
                upper = lax.broadcasted_iota(jnp.int32, (SUBLANES, half), 0) < SUM_ROW
                for c in range(2):
                    span = slice(c * half, (c + 1) * half)
                    obuf[finish, c, :HEAD_SIZE] = out[:, span]
                    obuf[finish, c, HEAD_SIZE:] = jnp.where(upper, top[:, span], total[:, span])

    def exchange_copy(u):
        return remote(obuf.at[u, 1 - core], xbuf.at[u], x_send.at[0], x_recv.at[u], sibling)

    def merge_cores(u):
        own_part, other_part = obuf[u, core, HEAD_SIZE:], xbuf[u, HEAD_SIZE:]
        top_a, top_b = own_part[:1], other_part[:1]
        sum_a, sum_b = own_part[SUM_ROW:SUM_ROW + 1], other_part[SUM_ROW:SUM_ROW + 1]
        top = jnp.maximum(top_a, top_b)
        scale_a = jnp.exp2((top_a - top) * EXP2_SCALE)
        scale_b = jnp.exp2((top_b - top) * EXP2_SCALE)
        total = sum_a * scale_a + sum_b * scale_b
        out = obuf[u, core, :HEAD_SIZE] * (scale_a / total) + xbuf[u, :HEAD_SIZE] * (scale_b / total)
        sbuf[u] = out.T.astype(BF16).reshape(tile_pairs, each, HEAD_SIZE)
        smbuf[u, 0:1] = top
        smbuf[u, 1:2] = total
        nbuf[u, my_place] = sbuf[u, my_place]
        nmbuf[u, my_place] = smbuf[u]

    def scatter(u):
        for j in range(1, tile_pairs):
            place = lax.rem(my_place + j, tile_pairs)
            remote(smbuf.at[u], nmbuf.at[u, my_place], nm_send.at[0], nm_recv.at[u], neighbour(j)).start()
            remote(sbuf.at[u, place], nbuf.at[u, my_place], n_send.at[0], n_recv.at[u], neighbour(j)).start()

    def await_scattered(u):
        await_bytes(nmbuf.at[u, pl.ds(0, tile_pairs - 1)], nm_recv.at[u])
        await_bytes(nbuf.at[u, pl.ds(0, tile_pairs - 1)], n_recv.at[u])

    def mix(tops, sums, parts):
        top = jnp.max(tops, axis=0, keepdims=True)
        weights = jnp.exp2((tops - top) * EXP2_SCALE) * sums
        total = jnp.sum(weights, axis=0, keepdims=True)
        weights = weights / total
        mine = jnp.zeros((len(parts), each), F32)
        for place in range(tile_pairs):
            mine = jnp.where(my_place == place, weights[:, place * each:(place + 1) * each], mine)
        diagonal = lax.broadcasted_iota(jnp.int32, (each, each), 0) == lax.broadcasted_iota(
            jnp.int32, (each, each), 1
        )
        result = jnp.zeros((each, HEAD_SIZE), F32)
        for source, part in enumerate(parts):
            line = jnp.broadcast_to(mine[source:source + 1, :], (each, each))
            column = jnp.sum(jnp.where(diagonal, line, 0.0), axis=1, keepdims=True)
            result = result + column * part.astype(F32)
        return result, top, total

    def merge_tile(u):
        h, _, tile = unit(u)
        await_scattered(u)
        result, top, total = mix(
            nmbuf[u, :, 0, :], nmbuf[u, :, 1, :], [nbuf[u, place] for place in range(tile_pairs)]
        )
        hbuf[h, tile] = result.astype(BF16)
        hmbuf[h, tile, 0:1] = top
        hmbuf[h, tile, 1:2] = total
        remote(
            hmbuf.at[h, tile], fmbuf.at[h, my_tile], farm_send.at[0], farm_recv.at[h], partner(tile)
        ).start()
        remote(hbuf.at[h, tile], fbuf.at[h, my_tile], far_send.at[0], far_recv.at[h], partner(tile)).start()

    def combine(h):
        u = near_unit(h)
        await_scattered(u)
        tops, sums = [nmbuf[u, :, 0, :]], [nmbuf[u, :, 1, :]]
        parts = [nbuf[u, place] for place in range(tile_pairs)]
        if tiles > 1:
            await_bytes(fmbuf.at[h, pl.ds(0, tiles - 1)], farm_recv.at[h])
            await_bytes(fbuf.at[h, pl.ds(0, tiles - 1)], far_recv.at[h])
        for step in range(1, tiles):
            tile = lax.rem(my_tile + step, tiles)
            tops.append(fmbuf[h, tile, 0:1])
            sums.append(fmbuf[h, tile, 1:2])
            parts.append(fbuf[h, tile])
        result, _, _ = mix(jnp.concatenate(tops, axis=0), jnp.concatenate(sums, axis=0), parts)
        for g in range(group):
            columns = pl.ds(pl.multiple_of((h * group + g) * HEAD_SIZE, HEAD_SIZE), HEAD_SIZE)
            out_ref[:, columns] = result[g * own:(g + 1) * own].astype(out_ref.dtype)

    def body(u, peeled=3):
        h, _, tile = unit(u)
        await_queries(u)

        @pl.when(u + 2 < heads)
        def _():
            k_copy(u + 2).start()
            v_copy(u + 2).start()

        if peeled > 2:
            exchange_copy(u - 3).wait_recv()
        if peeled > 0:
            for v in (2 * u + 2, 2 * u + 3):

                @pl.when(is_far(v))
                def _(v=v):
                    far_head, _, far_tile = unit(v)
                    await_block(far_head, far_tile)
                    forward(far_head, far_tile)

        @pl.when(u + 1 < units)
        def _():
            next_head, _, next_tile = unit(u + 1)
            relay(next_head, next_tile)

        if peeled > 2:

            @pl.when(is_far(u - 6))
            def _():
                merge_tile(u - 6)

        if peeled == 0:
            segment(None, (h, tile, 0))
        else:
            segment((unit(u - 1)[0], blocks - 1), (h, tile, 0), finish=u - 1)
        for b in range(1, blocks):
            segment((h, b - 1), (h, tile, b))
            if b == 1 and peeled > 2:
                merge_cores(u - 3)
        if peeled > 0:
            exchange_copy(u - 1).start()
        if peeled > 2:
            scatter(u - 3)

    pl.semaphore_wait(barrier, tile_devices - 1 + my_tile)
    for h in range(heads):
        await_block(h, my_tile)
    for h in range(early):
        forward(h, my_tile)
    lax.fori_loop(0, my_tile, lambda t, _: (signal(ready, partner(t)), 0)[1], 0)

    @pl.when(my_tile < tiles - 1)
    def _():
        pl.semaphore_wait(ready, tiles - 1 - my_tile)

    for step in range(1, tiles):
        tile = lax.rem(my_tile + step, tiles)
        for h in range(heads):
            mine = qbuf.at[h, my_tile, core, my_place]
            remote(mine, mine, far_query_send.at[0], block_recv.at[h, my_tile], partner(tile)).start()
    for h in range(early, heads):
        forward(h, my_tile)
    for u in range(early, min(4, late)):
        far_head, _, far_tile = unit(jnp.int32(u))
        await_block(far_head, far_tile)
        forward(far_head, far_tile)
    if heads > 1:
        k_copy(1).start()
        v_copy(1).start()
    first_head, _, first_tile = unit(jnp.int32(0))
    relay(first_head, first_tile)
    fk_copy.wait()
    fv_copy.wait()
    for u in range(min(3, units)):
        body(jnp.int32(u), u)
    lax.fori_loop(3, units, lambda u, _: (body(u), 0)[1], 0)

    def merge_and_scatter(u):
        exchange_copy(u).wait_recv()
        merge_cores(u)
        scatter(u)

    last = units - 1
    segment((unit(jnp.int32(last))[0], blocks - 1), None, finish=last)
    exchange_copy(last).start()
    for u in range(max(0, units - 3), last):
        merge_and_scatter(u)
    for u in range(max(early, units - 6), min(late, last)):
        merge_tile(jnp.int32(u))
    if late == units:
        merge_and_scatter(last)
        if tiles > 1:
            merge_tile(jnp.int32(last))
        lax.fori_loop(0, heads, lambda h, _: (combine(h), 0)[1], 0)
    else:
        lax.fori_loop(0, heads - 2, lambda h, _: (combine(h), 0)[1], 0)
        merge_and_scatter(last)
        lax.fori_loop(max(0, heads - 2), heads, lambda h, _: (combine(h), 0)[1], 0)

    await_bytes(sbuf.at[:, pl.ds(0, tile_pairs - 1)], gather_send.at[0])
    await_bytes(sbuf, relay_send.at[0])
    await_bytes(xbuf, x_send.at[0])
    await_bytes(nmbuf.at[:, pl.ds(0, tile_pairs - 1)], nm_send.at[0])
    await_bytes(nbuf.at[:, pl.ds(0, tile_pairs - 1)], n_send.at[0])
    if tiles > 1:
        await_bytes(fbuf.at[:, pl.ds(0, tiles - 1)], far_query_send.at[0])
        await_bytes(fmbuf.at[:, pl.ds(0, tiles - 1)], farm_send.at[0])
        await_bytes(fbuf.at[:, pl.ds(0, tiles - 1)], far_send.at[0])


def solution(mesh):
    devices = mesh.shape["ctx"]

    def shards(queries, cache_keys, prefix_values, incoming_keys, incoming_values):
        own = queries.shape[0]
        heads = cache_keys.shape[1] // HEAD_SIZE
        group = queries.shape[1] // cache_keys.shape[1]
        depth = cache_keys.shape[0]
        each = group * own
        pairs = devices // 2
        tile_pairs = min(pairs, TILE_ROWS // (2 * each))
        tiles = pairs // tile_pairs
        rows = 2 * tile_pairs * each
        units = heads * tiles
        block = min(BLOCK_KEYS, depth // 2)
        dma = pltpu.SemaphoreType.DMA
        return pl.pallas_call(
            functools.partial(kernel, devices, heads, group, own, block),
            out_shape=jax.ShapeDtypeStruct(queries.shape, queries.dtype),
            in_specs=[pl.BlockSpec(memory_space=pl.ANY)] * 5,
            out_specs=pl.BlockSpec(memory_space=pltpu.VMEM),
            scratch_shapes=[
                pltpu.VMEM((heads, tiles, 2, tile_pairs, each, HEAD_SIZE), BF16),
                pltpu.VMEM((heads, depth, HEAD_SIZE), BF16),
                pltpu.VMEM((heads, depth, HEAD_SIZE), BF16),
                pltpu.VMEM((own, heads * HEAD_SIZE), BF16),
                pltpu.VMEM((own, heads * HEAD_SIZE), BF16),
                pltpu.VMEM((block, rows), F32),
                pltpu.VMEM((block, rows), F32),
                pltpu.VMEM((own, rows), F32),
                pltpu.VMEM((own, rows), jnp.int32),
                pltpu.VMEM((2, SUBLANES, rows), F32),
                pltpu.VMEM((SUBLANES, rows), F32),
                pltpu.VMEM((SUBLANES, rows), F32),
                pltpu.VMEM((HEAD_SIZE, rows), F32),
                pltpu.VMEM((units, 2, HEAD_SIZE + SUBLANES, rows // 2), F32),
                pltpu.VMEM((units, HEAD_SIZE + SUBLANES, rows // 2), F32),
                pltpu.VMEM((units, tile_pairs, each, HEAD_SIZE), BF16),
                pltpu.VMEM((units, 2, rows // 2), F32),
                pltpu.VMEM((units, tile_pairs, each, HEAD_SIZE), BF16),
                pltpu.VMEM((units, tile_pairs, 2, rows // 2), F32),
                pltpu.VMEM((heads, tiles, each, HEAD_SIZE), BF16),
                pltpu.VMEM((heads, tiles, 2, rows // 2), F32),
                pltpu.VMEM((heads, tiles, each, HEAD_SIZE), BF16),
                pltpu.VMEM((heads, tiles, 2, rows // 2), F32),
                dma((heads,)), dma((heads,)), dma((2,)), pltpu.SemaphoreType.REGULAR,
                dma((heads, tiles)), dma((heads, tiles)), dma((heads, tiles)),
                dma((units,)), dma((units,)), dma((units,)), dma((heads,)), dma((heads,)),
                *[dma((1,))] * 8,
            ],
            compiler_params=pltpu.CompilerParams(
                collective_id=0, has_side_effects=True, vmem_limit_bytes=60 * 1024 * 1024
            ),
        )(queries, cache_keys, prefix_values, incoming_keys, incoming_values)

    spec = P("ctx", "head")
    return jax.shard_map(
        shards, mesh=mesh, in_specs=(spec,) * 5, out_specs=spec, check_vma=False
    )
```

time: 48.2 us -> 44.4 us (0.921)
  Pallas kernels: 46.6 us -> 42.8 us
    pallas_call x1, Pallas kernels: 46.6 us -> 42.8 us  [shards(): pl.pallas_call(functools.partial(kernel, devices, heads, group, own, bloc...]
where the time goes in v1:
time: 44.4 us; the launch traced here: 44.3 us
  Pallas kernels  42.8 us (96%)
  local copies, waits for them, and re-layouts  1.47 us (3%)
    pallas_call x1, Pallas kernels, shards(): pl.pallas_call(functools.partial(kernel, devices, heads, group, own, bloc...  42.8 us
    unnamed x1, local copies, waits for them, and re-layouts  1.47 us

profile of v1, /device:TPU:0, one launch (start us, length us, event | category | flops | bytes accessed | tf_op | source)
XLA Modules:
  0.0 44.3 jit_solution(17707350314292645896)
XLA Ops:
  0.0 42.8 %shard_map.55 = bf16[16,2048]{1,0:T(8,128)(2,1)} custom-call(bf16[16,2048]{1,0:T(8,128)(2,1)} %q_hbm.1, bf16[4096,1024]{1,0:T(8,128)(2,1)} %k_hbm.1, bf16[4096,1024]{1,0:T(8,128)(2,1)} %v_hbm.1, bf16[16,1024]{1,0:T(8,128)(2,1)} %fk_hbm.1, bf16[16,1024]{1,0:T(8,128)(2,1)} %fv_hbm.1), custom_call_target="tpu_custom_call" | custom-call | tf_op jit(solution)/shard_map/pallas_call | solution.py:421
  42.8 1.5 %copy.7 = bf16[16,2048]{1,0:T(8,128)(2,1)} copy(bf16[16,2048]{1,0:T(8,128)(2,1)} %shard_map.55) | data formatting | bytes 131072

commit v2 on v1

--- a/solution.py
+++ b/solution.py
@@ -12,6 +12,9 @@
 LANES = 128
 SUBLANES = 8
 SUM_ROW = 4
+STAT_ROWS = 16
+SUM_ROWS = 16
+LAG = 3
 TILE_ROWS = 256
 BLOCK_KEYS = 1024
 PIECE_KEYS = 256
@@ -24,8 +27,26 @@
     return lax.dot_general(a, b, (((1,), (1,)), ((), ())), preferred_element_type=F32)
 
 
-def tn_dot(a, b):
-    return lax.dot_general(a, b, (((0,), (0,)), ((), ())), preferred_element_type=F32)
+def weigh(values, weights):
+    ones = jnp.ones((SUM_ROWS, values.shape[0]), BF16)
+    return jnp.dot(jnp.concatenate([values.T, ones], axis=0), weights, preferred_element_type=F32)
+
+
+def stats_rows(top, total):
+    rows, parts = lax.broadcasted_iota(jnp.int32, (STAT_ROWS, top.shape[1]), 0), []
+    for value in (top, total):
+        high = value.astype(BF16).astype(F32)
+        middle = (value - high).astype(BF16).astype(F32)
+        parts += [high, middle, value - high - middle]
+    out = jnp.zeros(rows.shape, F32)
+    for i, part in enumerate(parts):
+        out = jnp.where(rows == i, part, out)
+    return out.astype(BF16)
+
+
+def read_stats(rows):
+    x = rows.astype(F32)
+    return x[0:1] + x[1:2] + x[2:3], x[3:4] + x[4:5] + x[5:6]
 
 
 def fold(x, op):
@@ -39,9 +60,9 @@
     devices, heads, group, own, block,
     q_hbm, k_hbm, v_hbm, fk_hbm, fv_hbm, out_ref,
     qbuf, kbuf, vbuf, fkbuf, fvbuf, scores_even, scores_odd, fresh_scores, relative,
-    block_max, row_max, row_sum, acc, obuf, xbuf, sbuf, smbuf, nbuf, nmbuf, hbuf, hmbuf, fbuf, fmbuf,
-    k_sem, v_sem, f_sem, ready, block_recv, gather_recv, relay_recv, x_recv, n_recv, nm_recv, far_recv, farm_recv,
-    far_query_send, gather_send, relay_send, x_send, n_send, nm_send, far_send, farm_send,
+    block_max, row_max, acc, obuf, xbuf, sbuf, nbuf, hbuf, fbuf, dbuf, lbuf,
+    k_sem, v_sem, f_sem, ready, block_recv, gather_recv, relay_recv, x_recv, n_recv, far_recv, d_recv,
+    far_query_send, gather_send, relay_send, x_send, n_send, far_send, d_send,
 ):
     tiles, tile_pairs = qbuf.shape[1], qbuf.shape[3]
     each = group * own
@@ -52,6 +73,8 @@
     units = heads * tiles
     early = heads // 2 if tiles > 1 else heads
     late = early + heads * (tiles - 1)
+    direct = min(2, heads - early if tiles > 1 else heads)
+    merged = units - direct
     me = lax.axis_index("ctx")
     core, pair = lax.rem(me, 2), lax.div(me, 2)
     my_tile, my_place = lax.div(pair, tile_pairs), lax.rem(pair, tile_pairs)
@@ -69,8 +92,11 @@
     def near_unit(h):
         return jnp.where(h < early, h, h + heads * (tiles - 1))
 
-    def neighbour(j):
-        return {"ctx": (my_tile * tile_pairs + lax.rem(my_place + j, tile_pairs)) * 2 + core}
+    def neighbour(j, other=0):
+        there = core if other == 0 else 1 - core
+        return {"ctx": (my_tile * tile_pairs + lax.rem(my_place + j, tile_pairs)) * 2 + there}
+
+    others = [(j, other) for j in range(tile_pairs - 1, -1, -1) for other in range(2) if j + other > 0]
 
     sibling = {"ctx": pair * 2 + 1 - core}
 
@@ -132,6 +158,14 @@
         for j in range(1, tile_pairs):
             remote(mine, mine, gather_send.at[0], gather_recv.at[h, tile], neighbour(j)).start()
 
+    def forward_to_all(h):
+        mine = qbuf.at[h, my_tile, core, my_place]
+        for j, other in others:
+            remote(mine, mine, gather_send.at[0], gather_recv.at[h, my_tile], neighbour(j, other)).start()
+
+    def await_all(h):
+        await_bytes(sbuf.at[pl.ds(0, len(others)), 0, pl.ds(0, each)], gather_recv.at[h, my_tile])
+
     def relay_copy(h, tile):
         mine = qbuf.at[h, tile, core]
         return remote(mine, mine, relay_send.at[0], relay_recv.at[h, tile], sibling)
@@ -140,9 +174,12 @@
         await_bytes(qbuf.at[h, tile, core, pl.ds(0, tile_pairs - 1)], gather_recv.at[h, tile])
         relay_copy(h, tile).start()
 
-    def await_queries(u):
+    def await_queries(u, peeled):
         h, step, tile = unit(u)
-        relay_copy(h, tile).wait_recv()
+        if peeled == 0 and early > 0:
+            await_all(0)
+        else:
+            relay_copy(h, tile).wait_recv()
 
         @pl.when((u < early) | ((step == 1) & (h >= early)))
         def _():
@@ -174,7 +211,7 @@
                 decay = jnp.exp2((before - top) * EXP2_SCALE)
             row_max[0:1] = top
             top8 = jnp.broadcast_to(top, (SUBLANES, rows))
-            weights, sums = [], []
+            weights = []
         if scores is not None:
             sh, tile, sb = scores
             queries = qbuf[sh, tile].reshape(rows, HEAD_SIZE)
@@ -184,7 +221,6 @@
                 s = score_slots[vb % 2][pl.ds(j * PIECE_KEYS, PIECE_KEYS), :]
                 s = s.reshape(PIECE_KEYS // SUBLANES, SUBLANES, rows)
                 p = jnp.exp2((s - top8[None]) * EXP2_SCALE)
-                sums.append(fold(p, jnp.add))
                 weights.append(p.reshape(PIECE_KEYS, rows).astype(BF16))
             if scores is not None:
                 tops.append(score_piece(sh, queries, sb, j))
@@ -193,21 +229,18 @@
                 tops.append(score_fresh(sh, tile, queries))
             block_max[sb % 2] = functools.reduce(jnp.maximum, tops)
         if values is not None:
-            out = tn_dot(vbuf[vh, pl.ds(vb * block, block), :], jnp.concatenate(weights, axis=0))
+            out = weigh(vbuf[vh, pl.ds(vb * block, block), :], jnp.concatenate(weights, axis=0))
             if vb == 0:
                 s = fresh_scores[...].reshape(own // SUBLANES, SUBLANES, rows)
                 p = jnp.exp2((s - top8[None]) * EXP2_SCALE)
-                sums.append(fold(p, jnp.add))
-                out = out + tn_dot(fvbuf[:, head_columns(vh)], p.reshape(own, rows).astype(BF16))
-            total = functools.reduce(jnp.add, sums)
+                out = out + weigh(fvbuf[:, head_columns(vh)], p.reshape(own, rows).astype(BF16))
             if vb > 0:
-                total = row_sum[...] * decay + total
                 out = acc[...] * decay + out
             if finish is None:
-                row_sum[...] = total
                 acc[...] = out
             else:
-                total = jnp.sum(total, axis=0, keepdims=True)
+                total = out[HEAD_SIZE:HEAD_SIZE + 1]
+                out = out[:HEAD_SIZE]
                 upper = lax.broadcasted_iota(jnp.int32, (SUBLANES, half), 0) < SUM_ROW
                 for c in range(2):
                     span = slice(c * half, (c + 1) * half)
@@ -226,23 +259,23 @@
         scale_b = jnp.exp2((top_b - top) * EXP2_SCALE)
         total = sum_a * scale_a + sum_b * scale_b
         out = obuf[u, core, :HEAD_SIZE] * (scale_a / total) + xbuf[u, :HEAD_SIZE] * (scale_b / total)
-        sbuf[u] = out.T.astype(BF16).reshape(tile_pairs, each, HEAD_SIZE)
-        smbuf[u, 0:1] = top
-        smbuf[u, 1:2] = total
+        sbuf[u, :, :each] = out.T.astype(BF16).reshape(tile_pairs, each, HEAD_SIZE)
+        stats = stats_rows(top, total)
+        for place in range(tile_pairs):
+            sbuf[u, place, each:] = stats
         nbuf[u, my_place] = sbuf[u, my_place]
-        nmbuf[u, my_place] = smbuf[u]
 
     def scatter(u):
         for j in range(1, tile_pairs):
             place = lax.rem(my_place + j, tile_pairs)
-            remote(smbuf.at[u], nmbuf.at[u, my_place], nm_send.at[0], nm_recv.at[u], neighbour(j)).start()
             remote(sbuf.at[u, place], nbuf.at[u, my_place], n_send.at[0], n_recv.at[u], neighbour(j)).start()
 
     def await_scattered(u):
-        await_bytes(nmbuf.at[u, pl.ds(0, tile_pairs - 1)], nm_recv.at[u])
         await_bytes(nbuf.at[u, pl.ds(0, tile_pairs - 1)], n_recv.at[u])
 
-    def mix(tops, sums, parts):
+    def mix(parts):
+        tops, sums = zip(*[read_stats(part[each:]) for part in parts], strict=True)
+        tops, sums = jnp.concatenate(tops, axis=0), jnp.concatenate(sums, axis=0)
         top = jnp.max(tops, axis=0, keepdims=True)
         weights = jnp.exp2((tops - top) * EXP2_SCALE) * sums
         total = jnp.sum(weights, axis=0, keepdims=True)
@@ -257,71 +290,82 @@
         for source, part in enumerate(parts):
             line = jnp.broadcast_to(mine[source:source + 1, :], (each, each))
             column = jnp.sum(jnp.where(diagonal, line, 0.0), axis=1, keepdims=True)
-            result = result + column * part.astype(F32)
+            result = result + column * part[:each].astype(F32)
         return result, top, total
 
     def merge_tile(u):
         h, _, tile = unit(u)
         await_scattered(u)
-        result, top, total = mix(
-            nmbuf[u, :, 0, :], nmbuf[u, :, 1, :], [nbuf[u, place] for place in range(tile_pairs)]
-        )
-        hbuf[h, tile] = result.astype(BF16)
-        hmbuf[h, tile, 0:1] = top
-        hmbuf[h, tile, 1:2] = total
-        remote(
-            hmbuf.at[h, tile], fmbuf.at[h, my_tile], farm_send.at[0], farm_recv.at[h], partner(tile)
-        ).start()
+        result, top, total = mix([nbuf[u, place] for place in range(tile_pairs)])
+        hbuf[h, tile, :each] = result.astype(BF16)
+        hbuf[h, tile, each:] = stats_rows(top, total)
         remote(hbuf.at[h, tile], fbuf.at[h, my_tile], far_send.at[0], far_recv.at[h], partner(tile)).start()
 
-    def combine(h):
-        u = near_unit(h)
-        await_scattered(u)
-        tops, sums = [nmbuf[u, :, 0, :]], [nmbuf[u, :, 1, :]]
-        parts = [nbuf[u, place] for place in range(tile_pairs)]
+    def send_direct(d):
+        u = merged + d
+        for c in range(2):
+            stats = obuf[u, c, HEAD_SIZE:]
+            top, total = stats[:1], stats[SUM_ROW:SUM_ROW + 1]
+            out = (obuf[u, c, :HEAD_SIZE] * (1.0 / total)).T.astype(BF16)
+            dbuf[d, c, :, :each] = out.reshape(tile_pairs, each, HEAD_SIZE)
+            stats = stats_rows(top, total)
+            for place in range(tile_pairs):
+                dbuf[d, c, place, each:] = stats
+        for j, other in others:
+            place = lax.rem(my_place + j, tile_pairs)
+            there = core if other == 0 else 1 - core
+            remote(
+                dbuf.at[d, there, place], lbuf.at[d, core, my_place], d_send.at[0], d_recv.at[d], neighbour(j, other)
+            ).start()
+        lbuf[d, core, my_place] = dbuf[d, core, my_place]
+
+    def direct_bytes(count):
+        return sbuf.at[pl.ds(0, count), 0]
+
+    def combine(h, d=None):
+        if d is None:
+            u = near_unit(h)
+            await_scattered(u)
+            parts = [nbuf[u, place] for place in range(tile_pairs)]
+        else:
+            await_bytes(direct_bytes(len(others)), d_recv.at[d])
+            parts = [lbuf[d, c, place] for c in range(2) for place in range(tile_pairs)]
         if tiles > 1:
-            await_bytes(fmbuf.at[h, pl.ds(0, tiles - 1)], farm_recv.at[h])
             await_bytes(fbuf.at[h, pl.ds(0, tiles - 1)], far_recv.at[h])
         for step in range(1, tiles):
-            tile = lax.rem(my_tile + step, tiles)
-            tops.append(fmbuf[h, tile, 0:1])
-            sums.append(fmbuf[h, tile, 1:2])
-            parts.append(fbuf[h, tile])
-        result, _, _ = mix(jnp.concatenate(tops, axis=0), jnp.concatenate(sums, axis=0), parts)
+            parts.append(fbuf[h, lax.rem(my_tile + step, tiles)])
+        result, _, _ = mix(parts)
         for g in range(group):
             columns = pl.ds(pl.multiple_of((h * group + g) * HEAD_SIZE, HEAD_SIZE), HEAD_SIZE)
             out_ref[:, columns] = result[g * own:(g + 1) * own].astype(out_ref.dtype)
 
-    def body(u, peeled=3):
+    def body(u, peeled=LAG):
         h, _, tile = unit(u)
-        await_queries(u)
-
-        @pl.when(u + 2 < heads)
-        def _():
-            k_copy(u + 2).start()
-            v_copy(u + 2).start()
-
-        if peeled > 2:
-            exchange_copy(u - 3).wait_recv()
-        if peeled > 0:
-            for v in (2 * u + 2, 2 * u + 3):
-
-                @pl.when(is_far(v))
-                def _(v=v):
-                    far_head, _, far_tile = unit(v)
-                    await_block(far_head, far_tile)
-                    forward(far_head, far_tile)
+        await_queries(u, peeled)
+
+        for n in {0: (2,), 1: (3, 4), 2: range(5, heads)}.get(peeled, ()):
+            if n < heads:
+                k_copy(n).start()
+                v_copy(n).start()
+
+        if peeled == LAG:
+            exchange_copy(u - LAG).wait_recv()
+        for v in {1: (4, 5), 2: range(6, late)}.get(peeled, ()):
+            if early <= v < late:
+                far_head, _, far_tile = unit(jnp.int32(v))
+                await_block(far_head, far_tile)
+                forward(far_head, far_tile)
 
         @pl.when(u + 1 < units)
         def _():
             next_head, _, next_tile = unit(u + 1)
             relay(next_head, next_tile)
 
-        if peeled > 2:
-
-            @pl.when(is_far(u - 6))
+        if peeled == LAG:
+
+            @pl.when(is_far(u - 2 * LAG))
             def _():
-                merge_tile(u - 6)
+                merge_tile(u - 2 * LAG)
 
         if peeled == 0:
             segment(None, (h, tile, 0))
@@ -329,18 +373,25 @@
             segment((unit(u - 1)[0], blocks - 1), (h, tile, 0), finish=u - 1)
         for b in range(1, blocks):
             segment((h, b - 1), (h, tile, b))
-            if b == 1 and peeled > 2:
-                merge_cores(u - 3)
+            if b == 1 and peeled == LAG:
+                merge_cores(u - LAG)
         if peeled > 0:
-            exchange_copy(u - 1).start()
-        if peeled > 2:
-            scatter(u - 3)
+
+            @pl.when(u - 1 < merged)
+            def _():
+                exchange_copy(u - 1).start()
+
+        if peeled == LAG:
+            scatter(u - LAG)
 
     pl.semaphore_wait(barrier, tile_devices - 1 + my_tile)
     for h in range(heads):
         await_block(h, my_tile)
     for h in range(early):
-        forward(h, my_tile)
+        if h == 0:
+            forward_to_all(h)
+        else:
+            forward(h, my_tile)
     lax.fori_loop(0, my_tile, lambda t, _: (signal(ready, partner(t)), 0)[1], 0)
 
     @pl.when(my_tile < tiles - 1)
@@ -361,13 +412,28 @@
     if heads > 1:
         k_copy(1).start()
         v_copy(1).start()
-    first_head, _, first_tile = unit(jnp.int32(0))
-    relay(first_head, first_tile)
+    if early == 0:
+        first_head, _, first_tile = unit(jnp.int32(0))
+        relay(first_head, first_tile)
     fk_copy.wait()
     fv_copy.wait()
-    for u in range(min(3, units)):
+    for u in range(min(LAG, units)):
         body(jnp.int32(u), u)
-    lax.fori_loop(3, units, lambda u, _: (body(u), 0)[1], 0)
+    lax.fori_loop(LAG, units, lambda u, _: (body(u), 0)[1], 0)
+
+    def drain():
+        forwards = units * (tile_pairs - 1) + (tile_pairs if early > 0 else 0)
+        relays = (units - 1 if early > 0 else units) * tile_pairs
+        await_bytes(kbuf.at[0, pl.ds(0, relays * each)], relay_send.at[0])
+        await_bytes(kbuf.at[0, pl.ds(0, forwards * each)], gather_send.at[0])
+        if merged > 0:
+            await_bytes(xbuf.at[pl.ds(0, merged)], x_send.at[0])
+            await_bytes(nbuf.at[pl.ds(0, merged), pl.ds(0, tile_pairs - 1)], n_send.at[0])
+        if tiles > 1:
+            await_bytes(qbuf.at[:, pl.ds(0, tiles - 1), 0, 0], far_query_send.at[0])
+            await_bytes(fbuf.at[:, pl.ds(0, tiles - 1)], far_send.at[0])
+        for d in range(direct):
+            await_bytes(direct_bytes(len(others)), d_send.at[0])
 
     def merge_and_scatter(u):
         exchange_copy(u).wait_recv()
@@ -375,31 +441,18 @@
         scatter(u)
 
     last = units - 1
+    if direct > 1:
+        send_direct(0)
     segment((unit(jnp.int32(last))[0], blocks - 1), None, finish=last)
-    exchange_copy(last).start()
-    for u in range(max(0, units - 3), last):
+    send_direct(direct - 1)
+    for u in range(max(0, units - LAG), merged):
         merge_and_scatter(u)
-    for u in range(max(early, units - 6), min(late, last)):
+    for u in range(max(early, units - 2 * LAG), late):
         merge_tile(jnp.int32(u))
-    if late == units:
-        merge_and_scatter(last)
-        if tiles > 1:
-            merge_tile(jnp.int32(last))
-        lax.fori_loop(0, heads, lambda h, _: (combine(h), 0)[1], 0)
-    else:
-        lax.fori_loop(0, heads - 2, lambda h, _: (combine(h), 0)[1], 0)
-        merge_and_scatter(last)
-        lax.fori_loop(max(0, heads - 2), heads, lambda h, _: (combine(h), 0)[1], 0)
-
-    await_bytes(sbuf.at[:, pl.ds(0, tile_pairs - 1)], gather_send.at[0])
-    await_bytes(sbuf, relay_send.at[0])
-    await_bytes(xbuf, x_send.at[0])
-    await_bytes(nmbuf.at[:, pl.ds(0, tile_pairs - 1)], nm_send.at[0])
-    await_bytes(nbuf.at[:, pl.ds(0, tile_pairs - 1)], n_send.at[0])
-    if tiles > 1:
-        await_bytes(fbuf.at[:, pl.ds(0, tiles - 1)], far_query_send.at[0])
-        await_bytes(fmbuf.at[:, pl.ds(0, tiles - 1)], farm_send.at[0])
-        await_bytes(fbuf.at[:, pl.ds(0, tiles - 1)], far_send.at[0])
+    lax.fori_loop(0, heads - direct, lambda h, _: (combine(h), 0)[1], 0)
+    drain()
+    for d in range(direct):
+        combine(heads - direct + d, d)
 
 
 def solution(mesh):
@@ -435,22 +488,19 @@
                 pltpu.VMEM((own, rows), jnp.int32),
                 pltpu.VMEM((2, SUBLANES, rows), F32),
                 pltpu.VMEM((SUBLANES, rows), F32),
-                pltpu.VMEM((SUBLANES, rows), F32),
-                pltpu.VMEM((HEAD_SIZE, rows), F32),
+                pltpu.VMEM((HEAD_SIZE + SUM_ROWS, rows), F32),
                 pltpu.VMEM((units, 2, HEAD_SIZE + SUBLANES, rows // 2), F32),
                 pltpu.VMEM((units, HEAD_SIZE + SUBLANES, rows // 2), F32),
-                pltpu.VMEM((units, tile_pairs, each, HEAD_SIZE), BF16),
-                pltpu.VMEM((units, 2, rows // 2), F32),
-                pltpu.VMEM((units, tile_pairs, each, HEAD_SIZE), BF16),
-                pltpu.VMEM((units, tile_pairs, 2, rows // 2), F32),
-                pltpu.VMEM((heads, tiles, each, HEAD_SIZE), BF16),
-                pltpu.VMEM((heads, tiles, 2, rows // 2), F32),
-                pltpu.VMEM((heads, tiles, each, HEAD_SIZE), BF16),
-                pltpu.VMEM((heads, tiles, 2, rows // 2), F32),
+                pltpu.VMEM((units, tile_pairs, each + STAT_ROWS, HEAD_SIZE), BF16),
+                pltpu.VMEM((units, tile_pairs, each + STAT_ROWS, HEAD_SIZE), BF16),
+                pltpu.VMEM((heads, tiles, each + STAT_ROWS, HEAD_SIZE), BF16),
+                pltpu.VMEM((heads, tiles, each + STAT_ROWS, HEAD_SIZE), BF16),
+                pltpu.VMEM((2, 2, tile_pairs, each + STAT_ROWS, HEAD_SIZE), BF16),
+                pltpu.VMEM((2, 2, tile_pairs, each + STAT_ROWS, HEAD_SIZE), BF16),
                 dma((heads,)), dma((heads,)), dma((2,)), pltpu.SemaphoreType.REGULAR,
                 dma((heads, tiles)), dma((heads, tiles)), dma((heads, tiles)),
-                dma((units,)), dma((units,)), dma((units,)), dma((heads,)), dma((heads,)),
-                *[dma((1,))] * 8,
+                dma((units,)), dma((units,)), dma((heads,)), dma((2,)),
+                *[dma((1,))] * 7,
             ],
             compiler_params=pltpu.CompilerParams(
                 collective_id=0, has_side_effects=True, vmem_limit_bytes=60 * 1024 * 1024

time: 44.4 us -> 43.1 us (0.971)
  Pallas kernels: 42.8 us -> 41.4 us
    pallas_call x1, Pallas kernels: 42.8 us -> 41.4 us  [shards(): pl.pallas_call(functools.partial(kernel, devices, heads, group, own, bloc...]
where the time goes in v2:
time: 43.1 us; the launch traced here: 42.9 us
  Pallas kernels  41.4 us (96%)
  local copies, waits for them, and re-layouts  1.47 us (3%)
    pallas_call x1, Pallas kernels, shards(): pl.pallas_call(functools.partial(kernel, devices, heads, group, own, bloc...  41.4 us
    unnamed x1, local copies, waits for them, and re-layouts  1.47 us

profile of v2, /device:TPU:0, one launch (start us, length us, event | category | flops | bytes accessed | tf_op | source)
XLA Modules:
  0.0 42.9 jit_solution(11697072397319808644)
XLA Ops:
  0.0 41.4 %shard_map.55 = bf16[16,2048]{1,0:T(8,128)(2,1)} custom-call(bf16[16,2048]{1,0:T(8,128)(2,1)} %q_hbm.1, bf16[4096,1024]{1,0:T(8,128)(2,1)} %k_hbm.1, bf16[4096,1024]{1,0:T(8,128)(2,1)} %v_hbm.1, bf16[16,1024]{1,0:T(8,128)(2,1)} %fk_hbm.1, bf16[16,1024]{1,0:T(8,128)(2,1)} %fv_hbm.1), custom_call_target="tpu_custom_call" | custom-call | tf_op jit(solution)/shard_map/pallas_call | solution.py:474
  41.5 1.5 %copy.7 = bf16[16,2048]{1,0:T(8,128)(2,1)} copy(bf16[16,2048]{1,0:T(8,128)(2,1)} %shard_map.55) | data formatting | bytes 131072

commit v3 on v2

--- a/solution.py
+++ b/solution.py
@@ -16,7 +16,7 @@
 SUM_ROWS = 16
 LAG = 3
 TILE_ROWS = 256
-BLOCK_KEYS = 1024
+BLOCK_KEYS = 2048
 PIECE_KEYS = 256
 EXP2_SCALE = 168.0 ** (-0.5) * math.log2(math.e)
 MASKED = -1e30
@@ -129,17 +129,21 @@
     def signal(sem, device):
         pl.semaphore_signal(sem, inc=1, device_id=device, device_id_type=pl.DeviceIdType.MESH)
 
-    for j in range(1, tile_devices):
-        signal(barrier, {"ctx": my_tile * tile_devices + lax.rem(lax.rem(me, tile_devices) + j, tile_devices)})
-    lax.fori_loop(my_tile + 1, tiles, lambda t, _: (signal(barrier, partner(t)), 0)[1], 0)
-
-    for h in range(heads):
+    def load_queries(h):
         for g in range(group):
             columns = pl.ds((h * group + g) * HEAD_SIZE, HEAD_SIZE)
             pltpu.make_async_copy(
                 q_hbm.at[:, columns], qbuf.at[h, my_tile, core, my_place, pl.ds(g * own, own)],
                 block_recv.at[h, my_tile],
             ).start()
+
+    load_queries(0)
+    for j in range(1, tile_devices):
+        signal(barrier, {"ctx": my_tile * tile_devices + lax.rem(lax.rem(me, tile_devices) + j, tile_devices)})
+    lax.fori_loop(my_tile + 1, tiles, lambda t, _: (signal(barrier, partner(t)), 0)[1], 0)
+
+    for h in range(1, heads):
+        load_queries(h)
     k_copy(0).start()
     fk_copy.start()
     fv_copy.start()
@@ -385,14 +389,16 @@
             scatter(u - LAG)
 
     pl.semaphore_wait(barrier, tile_devices - 1 + my_tile)
-    for h in range(heads):
+    for h in range(early):
         await_block(h, my_tile)
-    for h in range(early):
         if h == 0:
             forward_to_all(h)
         else:
             forward(h, my_tile)
     lax.fori_loop(0, my_tile, lambda t, _: (signal(ready, partner(t)), 0)[1], 0)
+
+    for h in range(early, heads):
+        await_block(h, my_tile)
 
     @pl.when(my_tile < tiles - 1)
     def _():

time: 43.1 us -> 42.7 us (level)
  no operation moved by 1% of the time
where the time goes in v3:
time: 42.7 us; the launch traced here: 42.6 us
  Pallas kernels  41.1 us (96%)
  local copies, waits for them, and re-layouts  1.47 us (3%)
    pallas_call x1, Pallas kernels, shards(): pl.pallas_call(functools.partial(kernel, devices, heads, group, own, bloc...  41.1 us
    unnamed x1, local copies, waits for them, and re-layouts  1.47 us

profile of v3, /device:TPU:0, one launch (start us, length us, event | category | flops | bytes accessed | tf_op | source)
XLA Modules:
  0.0 42.6 jit_solution(14898946462594400440)
XLA Ops:
  0.0 41.1 %shard_map.55 = bf16[16,2048]{1,0:T(8,128)(2,1)} custom-call(bf16[16,2048]{1,0:T(8,128)(2,1)} %q_hbm.1, bf16[4096,1024]{1,0:T(8,128)(2,1)} %k_hbm.1, bf16[4096,1024]{1,0:T(8,128)(2,1)} %v_hbm.1, bf16[16,1024]{1,0:T(8,128)(2,1)} %fk_hbm.1, bf16[16,1024]{1,0:T(8,128)(2,1)} %fv_hbm.1), custom_call_target="tpu_custom_call" | custom-call | tf_op jit(solution)/shard_map/pallas_call | solution.py:480
  41.1 1.5 %copy.7 = bf16[16,2048]{1,0:T(8,128)(2,1)} copy(bf16[16,2048]{1,0:T(8,128)(2,1)} %shard_map.55) | data formatting | bytes 131072
